TPU v7x, 32 devices: a whole 2x2x4 slice. The times are simulated.
32 devices in a mesh: gx: 8 (over z, core), gz: 4 (over y, x).
Axes of the slice: x: 2, y: 2, z: 4, core: 2. Of those that a mesh axis runs over, the one named last changes fastest.
Arguments:
- populations: float32 [19, 8, 32, 1024], P(None, None, 'gz', 'gx'), may hold values from 0.001 to 0.6, as said below
- solid: int32 [8, 32, 1024], P(None, 'gz', 'gx'), may hold values from 0 to 1, as said below
- top_inflow: float32 [5, 32, 1024], P(None, 'gz', 'gx'), may hold values from 0.005 to 0.1
Outputs:
- advanced: float32 [19, 8, 32, 1024], P(None, None, 'gz', 'gx')
Inputs may be any that keep to these rules, and one draw needn't show every extreme that they name: Positive populations near equilibrium. Only the two planes nearest the wall hold solid nodes.
All inputs are finite; a program needn't handle non-finite values.
Results may differ from a plain program's by a relative error of at most 0.0003.
Values sent between devices are 32-bit elements; how exact they have to be, the bound alone decides.
A program may use at most 64 MiB of HBM per device.

v0:
```python
from functools import reduce
import jax
import jax.numpy as jnp
import numpy as np
from jax import lax
from jax.sharding import PartitionSpec as P

STEPS = 2
lattice = np.array(
    [
        [0, 0, 0],
        [1, 0, 0],
        [-1, 0, 0],
        [0, 1, 0],
        [0, -1, 0],
        [0, 0, 1],
        [0, 0, -1],
        [1, 1, 0],
        [-1, -1, 0],
        [1, -1, 0],
        [-1, 1, 0],
        [1, 0, 1],
        [-1, 0, -1],
        [1, 0, -1],
        [-1, 0, 1],
        [0, 1, 1],
        [0, -1, -1],
        [0, 1, -1],
        [0, -1, 1],
    ]
)
lattice_weights = [1.0 / 3.0] + [1.0 / 18.0] * 6 + [1.0 / 36.0] * 12
opposite = [0, 2, 1, 4, 3, 6, 5, 8, 7, 10, 9, 12, 11, 14, 13, 16, 15, 18, 17]
incoming = [4, 8, 9, 16, 18]
base_drive = 0.0001
drive_gain = 1.0
target_flow = 0.1


def extended(block, sides, width):
    for axis, dim in sides:
        count = lax.axis_size(axis)
        forward = [(i, i + 1) for i in range(count - 1)]
        forward.append((count - 1, 0))
        backward = [(target, source) for source, target in forward]
        low = lax.ppermute(
            lax.slice_in_dim(block, block.shape[dim] - width, None, axis=dim), axis, forward
        )
        high = lax.ppermute(lax.slice_in_dim(block, 0, width, axis=dim), axis, backward)
        block = jnp.concatenate([low, block, high], axis=dim)
    return block


def invert_rows(matrix):
    order = len(matrix)
    work = [
        list(matrix[row]) + [1.0 if col == row else 0.0 for col in range(order)]
        for row in range(order)
    ]
    for col in range(order):
        pivot = max(range(col, order), key=lambda row: abs(work[row][col]))
        work[col], work[pivot] = (work[pivot], work[col])
        lead = work[col][col]
        work[col] = [value / lead for value in work[col]]
        for row in range(order):
            if row != col:
                factor = work[row][col]
                if factor != 0.0:
                    work[row] = [
                        value - factor * other for value, other in zip(work[row], work[col])
                    ]
    return [line[order:] for line in work]


def collide_matrix():
    moment_rows = []
    for power in [
        (0, 0, 0),
        (1, 0, 0),
        (0, 1, 0),
        (0, 0, 1),
        (1, 1, 0),
        (1, 0, 1),
        (0, 1, 1),
        (2, 0, 0),
        (0, 2, 0),
        (0, 0, 2),
        (1, 2, 0),
        (1, 0, 2),
        (2, 1, 0),
        (0, 1, 2),
        (2, 0, 1),
        (0, 2, 1),
        (2, 2, 0),
        (2, 0, 2),
        (0, 2, 2),
    ]:
        moment_rows.append(
            [
                float(
                    int(lattice[q, 0]) ** power[0]
                    * int(lattice[q, 1]) ** power[1]
                    * int(lattice[q, 2]) ** power[2]
                )
                for q in range(19)
            ]
        )
    rates = [0.0] * 4 + [1.8] * 6 + [1.2] * 6 + [1.1] * 3
    inverse = invert_rows(moment_rows)
    result = [
        [
            sum((inverse[row][mid] * rates[mid] * moment_rows[mid][col] for mid in range(19)))
            for col in range(19)
        ]
        for row in range(19)
    ]
    return np.array(result, dtype=np.float32)


def signed_sum(populations, component):
    plus_terms = [populations[index] for index in range(19) if lattice[index, component] == 1]
    minus_terms = [populations[index] for index in range(19) if lattice[index, component] == -1]
    return reduce(lambda left, right: left + right, plus_terms) - reduce(
        lambda left, right: left + right, minus_terms
    )


def moments(populations):
    density = jnp.sum(populations, axis=0)
    momentum = (signed_sum(populations, 0), signed_sum(populations, 1), signed_sum(populations, 2))
    return (density, momentum)


def project(index, velocity):
    result = jnp.zeros_like(velocity[0])
    for component in range(3):
        factor = int(lattice[index, component])
        if factor == 1:
            result = result + velocity[component]
        elif factor == -1:
            result = result - velocity[component]
    return result


def equilibrium(density, velocity):
    speed_square = velocity[0] * velocity[0] + velocity[1] * velocity[1] + velocity[2] * velocity[2]
    terms = []
    for index in range(19):
        along = project(index, velocity)
        terms.append(
            lattice_weights[index]
            * density
            * (1.0 + 3.0 * along + 4.5 * along * along - 1.5 * speed_square)
        )
    return jnp.stack(terms)


def collide(current, density, momentum, driving):
    velocity = tuple((part_value / density for part_value in momentum))
    base_state = equilibrium(density, velocity)
    pushed = equilibrium(density, (velocity[0] + driving / density, velocity[1], velocity[2]))
    relaxed = jnp.tensordot(
        jnp.asarray(collide_matrix()), current - base_state, axes=1, precision=lax.Precision.HIGHEST
    )
    return current - relaxed + pushed - base_state


def extend(collided):
    return extended(collided, (("gx", 3), ("gz", 2)), 1)


def shift_planes(carried, blocked, step_y):
    if step_y == 1:
        carried = jnp.concatenate([jnp.zeros_like(carried[:1]), carried[:-1]], axis=0)
        blocked = jnp.concatenate([jnp.ones_like(blocked[:1]), blocked[:-1]], axis=0)
    elif step_y == -1:
        carried = jnp.concatenate([carried[1:], jnp.zeros_like(carried[:1])], axis=0)
        blocked = jnp.concatenate([blocked[1:], jnp.zeros_like(blocked[:1])], axis=0)
    return (carried, blocked)


def trim(array, cut):
    if cut == 0:
        return array
    return array[..., cut:-cut, cut:-cut]


def stream_block(padded, solid_padded, top_inflow, before):
    planes = padded.shape[1]
    width_z = padded.shape[2] - 2
    width_x = padded.shape[3] - 2
    collided = trim(padded, 1)
    solid = trim(solid_padded, 1)
    results = []
    for index in range(19):
        step_x = int(lattice[index, 0])
        step_y = int(lattice[index, 1])
        step_z = int(lattice[index, 2])
        carried = padded[
            index, :, 1 - step_z : 1 - step_z + width_z, 1 - step_x : 1 - step_x + width_x
        ]
        blocked = solid_padded[
            :, 1 - step_z : 1 - step_z + width_z, 1 - step_x : 1 - step_x + width_x
        ]
        carried, blocked = shift_planes(carried, blocked, step_y)
        arrived = jnp.where(blocked == 1, collided[opposite[index]], carried)
        if step_y == -1:
            arrived = arrived.at[planes - 1].set(top_inflow[incoming.index(index)])
        results.append(arrived)
    return jnp.where(solid[None] == 1, before, jnp.stack(results))


def total_flow(local_sum, node_total):
    return lax.psum(local_sum, ("gx", "gz")) / node_total


def local(populations, solid, top_inflow):
    node_total = float(
        populations.shape[1]
        * populations.shape[2]
        * populations.shape[3]
        * lax.axis_size("gx")
        * lax.axis_size("gz")
    )
    fluid_nodes = (1 - solid).astype(jnp.float32)
    solid_padded = extended(solid, (("gx", 2), ("gz", 1)), 1)
    current = populations
    for step_index in range(STEPS):
        density, momentum = moments(current)
        local_sum = jnp.sum(momentum[0] * fluid_nodes)
        bulk_flow = total_flow(local_sum, node_total)
        driving = base_drive + drive_gain * (target_flow - bulk_flow)
        collided = collide(current, density, momentum, driving)
        padded = extend(collided)
        current = stream_block(padded, solid_padded, top_inflow, current)
    return current


def solution(mesh):
    return jax.shard_map(
        local,
        mesh=mesh,
        in_specs=(P(None, None, "gz", "gx"), P(None, "gz", "gx"), P(None, "gz", "gx")),
        out_specs=P(None, None, "gz", "gx"),
        check_vma=False,
    )
```

profile of v0, /device:TPU:0, one launch (start us, length us, event | category | flops | bytes accessed | tf_op | source)
XLA Modules:
  0.0 149.5 jit_solution(2305365441169737833)
XLA Ops:
  0.0 1.0 fusion.266
  1.0 4.5 %collective-permute-start.2 = (s32[8,8,1]{2,1,0:T(8,128)S(1)}, s32[8,8,1]{2,1,0:T(8,128)S(1)}, u32[]{:S(2)}, u32[]{:S(2)}) collective-permute-start(s32[8,8,1]{2,1,0:T(8,128)S(1)} %get-tuple-element.284), channel_id=1, source_target_pairs={{4,0},{8,4},{12,8},{16,12},{20,16},{24,20},{28,24},{0,28},{5,1},{9... | collective-permute-start | bytes 776 | tf_op jit(solution)/shard_map/ppermute | solution.py:49
  5.5 1.5 %fusion.243 = (f32[]{:T(128)}, f32[1,8,8,128]{3,2,1,0:T(8,128)S(1)}) fusion(s32[8,8,128]{2,1,0:T(8,128)S(1)} %copy-done.1, f32[19,8,8,128]{3,2,1,0:T(8,128)} %param.25), kind=kLoop, calls=%fused_computation.503 | loop fusion | flops 106495 | bytes 393220 | tf_op jit(solution)/shard_map/reduce_sum | solution.py:230
  7.0 1.1 reduce_sum.40
  8.2 39.1 %psum.14 = f32[]{:T(128)} all-reduce(f32[]{:T(128)} %get-tuple-element.179), channel_id=1, replica_groups=mesh['gx'=8,'gz'=4] {'gx','gz'}, use_global_device_ids=true, to_apply=%region_2.0 | all-reduce | flops 1 | bytes 8 | tf_op jit(solution)/shard_map/psum | solution.py:214
  49.4 1.1 fusion.2
  50.9 1.2 copy.80
  52.6 3.6 %collective-permute-start.3 = (f32[19,8,8,1]{0,2,3,1:T(8,128)S(1)}, f32[19,8,8,1]{0,2,3,1:T(8,128)S(1)}, u32[]{:S(2)}, u32[]{:S(2)}) collective-permute-start(f32[19,8,8,1]{0,2,3,1:T(8,128)S(1)} %copy.82), channel_id=1, source_target_pairs={{4,0},{8,4},{12,8},{16,12},{20,16},{24,20},{28,24},{0,28},{5,1},{9... | collective-permute-start | bytes 14600 | tf_op jit(solution)/shard_map/ppermute | solution.py:49
  56.4 3.4 %collective-permute-start.6 = (s32[8,1,130]{2,1,0:T(1,128)S(1)}, s32[8,1,130]{2,1,0:T(1,128)S(1)}, u32[]{:S(2)}, u32[]{:S(2)}) collective-permute-start(s32[8,1,130]{2,1,0:T(1,128)S(1)} %get-tuple-element.242), channel_id=1, source_target_pairs={{1,0},{2,1},{3,2},{0,3},{5,4},{6,5},{7,6},{4,7},{9,8},{10,9},{11,1... | collective-permute-start | bytes 12488 | tf_op jit(solution)/shard_map/ppermute | solution.py:49
  61.2 3.1 %collective-permute-done.4 = s32[8,1,130]{2,1,0:T(1,128)S(1)} collective-permute-done((s32[8,1,130]{2,1,0:T(1,128)S(1)}, s32[8,1,130]{2,1,0:T(1,128)S(1)}, u32[]{:S(2)}, u32[]{:S(2)}) %collective-permute-start.4) | collective-permute-done | bytes 4192 | tf_op jit(solution)/shard_map/ppermute | solution.py:46
  65.9 1.5 copy.81
  67.5 1.0 pad_maximum_fusion.3
  69.3 2.0 %collective-permute-start.5 = (f32[19,8,1,130]{3,2,1,0:T(1,128)S(1)}, f32[19,8,1,130]{3,2,1,0:T(1,128)S(1)}, u32[]{:S(2)}, u32[]{:S(2)}) collective-permute-start(f32[19,8,1,130]{3,2,1,0:T(1,128)S(1)} %get-tuple-element.198), channel_id=1, source_target_pairs={{0,1},{1,2},{2,3},{3,0},{4,5},{5,6},{6,7},{7,4},{8,9},{9,10},{10,1... | collective-permute-start | bytes 237128 | tf_op jit(solution)/shard_map/ppermute | solution.py:46
  71.9 2.6 %collective-permute-done.7 = f32[19,8,1,130]{3,2,1,0:T(1,128)S(1)} collective-permute-done((f32[19,8,1,130]{3,2,1,0:T(1,128)S(1)}, f32[19,8,1,130]{3,2,1,0:T(1,128)S(1)}, u32[]{:S(2)}, u32[]{:S(2)}) %collective-permute-start.7) | collective-permute-done | bytes 79072 | tf_op jit(solution)/shard_map/ppermute | solution.py:49
  74.5 1.5 %collective-permute-done.5 = f32[19,8,1,130]{3,2,1,0:T(1,128)S(1)} collective-permute-done((f32[19,8,1,130]{3,2,1,0:T(1,128)S(1)}, f32[19,8,1,130]{3,2,1,0:T(1,128)S(1)}, u32[]{:S(2)}, u32[]{:S(2)}) %collective-permute-start.5) | collective-permute-done | bytes 79072 | tf_op jit(solution)/shard_map/ppermute | solution.py:46
  83.5 38.8 %psum.15 = f32[]{:T(128)} all-reduce(f32[]{:T(128)} %get-tuple-element.131), channel_id=1, replica_groups=mesh['gx'=8,'gz'=4] {'gx','gz'}, use_global_device_ids=true, to_apply=%region_5.6 | all-reduce | flops 1 | bytes 8 | tf_op jit(solution)/shard_map/psum | solution.py:214
  124.5 1.1 fusion
  127.2 3.5 %collective-permute-start.9 = (f32[19,8,8,1]{0,2,3,1:T(8,128)S(1)}, f32[19,8,8,1]{0,2,3,1:T(8,128)S(1)}, u32[]{:S(2)}, u32[]{:S(2)}) collective-permute-start(f32[19,8,8,1]{0,2,3,1:T(8,128)S(1)} %copy.90), channel_id=1, source_target_pairs={{4,0},{8,4},{12,8},{16,12},{20,16},{24,20},{28,24},{0,28},{5,1},{9... | collective-permute-start | bytes 14600 | tf_op jit(solution)/shard_map/ppermute | solution.py:49
  131.3 1.0 collective-permute-done.9
  133.9 1.0 pad_maximum_fusion
  134.9 3.6 %collective-permute-start.11 = (f32[19,8,1,130]{3,2,1,0:T(1,128)S(1)}, f32[19,8,1,130]{3,2,1,0:T(1,128)S(1)}, u32[]{:S(2)}, u32[]{:S(2)}) collective-permute-start(f32[19,8,1,130]{3,2,1,0:T(1,128)S(1)} %get-tuple-element.193), channel_id=1, source_target_pairs={{1,0},{2,1},{3,2},{0,3},{5,4},{6,5},{7,6},{4,7},{9,8},{10,9},{11,1... | collective-permute-start | bytes 237128 | tf_op jit(solution)/shard_map/ppermute | solution.py:49
  139.9 3.0 %collective-permute-done.11 = f32[19,8,1,130]{3,2,1,0:T(1,128)S(1)} collective-permute-done((f32[19,8,1,130]{3,2,1,0:T(1,128)S(1)}, f32[19,8,1,130]{3,2,1,0:T(1,128)S(1)}, u32[]{:S(2)}, u32[]{:S(2)}) %collective-permute-start.11) | collective-permute-done | bytes 79072 | tf_op jit(solution)/shard_map/ppermute | solution.py:49
  142.9 2.8 %collective-permute-done.10 = f32[19,8,1,130]{3,2,1,0:T(1,128)S(1)} collective-permute-done((f32[19,8,1,130]{3,2,1,0:T(1,128)S(1)}, f32[19,8,1,130]{3,2,1,0:T(1,128)S(1)}, u32[]{:S(2)}, u32[]{:S(2)}) %collective-permute-start.10) | collective-permute-done | bytes 79072 | tf_op jit(solution)/shard_map/ppermute | solution.py:46
  148.5 0.9 broadcast_select_fusion
  (178 shorter events, 23.5 us)
Async XLA Ops:
  0.0 5.5 %copy-start.1 = (s32[8,8,128]{2,1,0:T(8,128)S(1)}, s32[8,8,128]{2,1,0:T(8,128)}, u32[]{:S(2)}) copy-start(s32[8,8,128]{2,1,0:T(8,128)} %param.26) | copy-start | bytes 98308
  0.0 47.9 %copy-start = (f32[19,8,8,128]{3,2,1,0:T(8,128)S(1)}, f32[19,8,8,128]{3,2,1,0:T(8,128)}, u32[]{:S(2)}) copy-start(f32[19,8,8,128]{3,2,1,0:T(8,128)} %param.25) | copy-start | bytes 1867780
  1.0 55.3 %collective-permute-start.2 = (s32[8,8,1]{2,1,0:T(8,128)S(1)}, s32[8,8,1]{2,1,0:T(8,128)S(1)}, u32[]{:S(2)}, u32[]{:S(2)}) collective-permute-start(s32[8,8,1]{2,1,0:T(8,128)S(1)} %get-tuple-element.284), channel_id=1, source_target_pairs={{4,0},{8,4},{12,8},{16,12},{20,16},{24,20},{28,24},{0,28},{5,1},{9... | collective-permute-start | bytes 776 | tf_op jit(solution)/shard_map/ppermute | solution.py:49
  5.5 50.7 %collective-permute-start = (s32[8,8,1]{2,1,0:T(8,128)S(1)}, s32[8,8,1]{2,1,0:T(8,128)S(1)}, u32[]{:S(2)}, u32[]{:S(2)}) collective-permute-start(s32[8,8,1]{2,1,0:T(8,128)S(1)} %get-tuple-element.285), channel_id=1, source_target_pairs={{0,4},{4,8},{8,12},{12,16},{16,20},{20,24},{24,28},{28,0},{1,5},{5... | collective-permute-start | bytes 776 | tf_op jit(solution)/shard_map/ppermute | solution.py:46
  52.1 13.8 %collective-permute-start.1 = (f32[19,8,8,1]{0,2,3,1:T(8,128)}, f32[19,8,8,1]{0,2,3,1:T(8,128)}, u32[]{:S(2)}, u32[]{:S(2)}) collective-permute-start(f32[19,8,8,1]{0,2,3,1:T(8,128)} %copy.80), channel_id=1, source_target_pairs={{0,4},{4,8},{8,12},{12,16},{16,20},{20,24},{24,28},{28,0},{1,5},{5... | collective-permute-start | bytes 14600 | tf_op jit(solution)/shard_map/ppermute | solution.py:46
  52.6 12.6 %collective-permute-start.3 = (f32[19,8,8,1]{0,2,3,1:T(8,128)S(1)}, f32[19,8,8,1]{0,2,3,1:T(8,128)S(1)}, u32[]{:S(2)}, u32[]{:S(2)}) collective-permute-start(f32[19,8,8,1]{0,2,3,1:T(8,128)S(1)} %copy.82), channel_id=1, source_target_pairs={{4,0},{8,4},{12,8},{16,12},{20,16},{24,20},{28,24},{0,28},{5,1},{9... | collective-permute-start | bytes 14600 | tf_op jit(solution)/shard_map/ppermute | solution.py:49
  56.4 4.8 %collective-permute-start.6 = (s32[8,1,130]{2,1,0:T(1,128)S(1)}, s32[8,1,130]{2,1,0:T(1,128)S(1)}, u32[]{:S(2)}, u32[]{:S(2)}) collective-permute-start(s32[8,1,130]{2,1,0:T(1,128)S(1)} %get-tuple-element.242), channel_id=1, source_target_pairs={{1,0},{2,1},{3,2},{0,3},{5,4},{6,5},{7,6},{4,7},{9,8},{10,9},{11,1... | collective-permute-start | bytes 12488 | tf_op jit(solution)/shard_map/ppermute | solution.py:49
  59.7 4.5 %collective-permute-start.4 = (s32[8,1,130]{2,1,0:T(1,128)S(1)}, s32[8,1,130]{2,1,0:T(1,128)S(1)}, u32[]{:S(2)}, u32[]{:S(2)}) collective-permute-start(s32[8,1,130]{2,1,0:T(1,128)S(1)} %get-tuple-element.243), channel_id=1, source_target_pairs={{0,1},{1,2},{2,3},{3,0},{4,5},{5,6},{6,7},{7,4},{8,9},{9,10},{10,1... | collective-permute-start | bytes 12488 | tf_op jit(solution)/shard_map/ppermute | solution.py:46
  68.6 2.7 %copy-start.12 = (s32[7,8,128]{2,1,0:T(8,128)S(1)}, s32[7,8,128]{2,1,0:T(8,128)}, u32[]{:S(2)}) copy-start(s32[7,8,128]{2,1,0:T(8,128)} %get-tuple-element.282) | copy-start | bytes 86020
  69.3 5.2 %collective-permute-start.7 = (f32[19,8,1,130]{3,2,1,0:T(1,128)S(1)}, f32[19,8,1,130]{3,2,1,0:T(1,128)S(1)}, u32[]{:S(2)}, u32[]{:S(2)}) collective-permute-start(f32[19,8,1,130]{3,2,1,0:T(1,128)S(1)} %get-tuple-element.197), channel_id=1, source_target_pairs={{1,0},{2,1},{3,2},{0,3},{5,4},{6,5},{7,6},{4,7},{9,8},{10,9},{11,1... | collective-permute-start | bytes 237128 | tf_op jit(solution)/shard_map/ppermute | solution.py:49
  69.3 6.7 %collective-permute-start.5 = (f32[19,8,1,130]{3,2,1,0:T(1,128)S(1)}, f32[19,8,1,130]{3,2,1,0:T(1,128)S(1)}, u32[]{:S(2)}, u32[]{:S(2)}) collective-permute-start(f32[19,8,1,130]{3,2,1,0:T(1,128)S(1)} %get-tuple-element.198), channel_id=1, source_target_pairs={{0,1},{1,2},{2,3},{3,0},{4,5},{5,6},{6,7},{7,4},{8,9},{9,10},{10,1... | collective-permute-start | bytes 237128 | tf_op jit(solution)/shard_map/ppermute | solution.py:46
  76.1 0.7 copy-start.6
  76.1 0.8 copy-start.7
  76.1 0.8 copy-start.8
  76.1 0.8 copy-start.10
  76.1 0.8 copy-start.11
  78.3 0.7 copy-start.9
  81.3 0.7 copy-start.4
  82.0 0.7 copy-start.3
  127.1 5.9 %collective-permute-start.8 = (f32[19,8,8,1]{0,2,3,1:T(8,128)S(1)}, f32[19,8,8,1]{0,2,3,1:T(8,128)S(1)}, u32[]{:S(2)}, u32[]{:S(2)}) collective-permute-start(f32[19,8,8,1]{0,2,3,1:T(8,128)S(1)} %copy.88), channel_id=1, source_target_pairs={{0,4},{4,8},{8,12},{12,16},{16,20},{20,24},{24,28},{28,0},{1,5},{5... | collective-permute-start | bytes 14600 | tf_op jit(solution)/shard_map/ppermute | solution.py:46
  127.2 5.1 %collective-permute-start.9 = (f32[19,8,8,1]{0,2,3,1:T(8,128)S(1)}, f32[19,8,8,1]{0,2,3,1:T(8,128)S(1)}, u32[]{:S(2)}, u32[]{:S(2)}) collective-permute-start(f32[19,8,8,1]{0,2,3,1:T(8,128)S(1)} %copy.90), channel_id=1, source_target_pairs={{4,0},{8,4},{12,8},{16,12},{20,16},{24,20},{28,24},{0,28},{5,1},{9... | collective-permute-start | bytes 14600 | tf_op jit(solution)/shard_map/ppermute | solution.py:49
  133.8 4.7 %copy-start.2 = (f32[19,8,8,128]{3,2,1,0:T(8,128)S(1)}, f32[19,8,8,128]{3,2,1,0:T(8,128)}, u32[]{:S(2)}) copy-start(f32[19,8,8,128]{3,2,1,0:T(8,128)} %constant_dynamic-update-slice_fusion.115) | copy-start | bytes 1867780
  134.9 8.0 %collective-permute-start.11 = (f32[19,8,1,130]{3,2,1,0:T(1,128)S(1)}, f32[19,8,1,130]{3,2,1,0:T(1,128)S(1)}, u32[]{:S(2)}, u32[]{:S(2)}) collective-permute-start(f32[19,8,1,130]{3,2,1,0:T(1,128)S(1)} %get-tuple-element.193), channel_id=1, source_target_pairs={{1,0},{2,1},{3,2},{0,3},{5,4},{6,5},{7,6},{4,7},{9,8},{10,9},{11,1... | collective-permute-start | bytes 237128 | tf_op jit(solution)/shard_map/ppermute | solution.py:49
  138.5 7.2 %collective-permute-start.10 = (f32[19,8,1,130]{3,2,1,0:T(1,128)S(1)}, f32[19,8,1,130]{3,2,1,0:T(1,128)S(1)}, u32[]{:S(2)}, u32[]{:S(2)}) collective-permute-start(f32[19,8,1,130]{3,2,1,0:T(1,128)S(1)} %get-tuple-element.194), channel_id=1, source_target_pairs={{0,1},{1,2},{2,3},{3,0},{4,5},{5,6},{6,7},{7,4},{8,9},{9,10},{10,1... | collective-permute-start | bytes 237128 | tf_op jit(solution)/shard_map/ppermute | solution.py:46
  (10 other events, 7.1 us)
where the time goes:
time: 151 us; the launch traced here: 149 us
  blocking collectives  77.9 us (52%)
  starting transfers between devices  20.7 us (14%)
  local copies, waits for them, and re-layouts  17.8 us (12%)
  other arithmetic  14.9 us (10%)
  waiting for transfers between devices  14 us (9%)
  matrix products  2.11 us (1%)
  between operations  2.08 us (1%)
    psum x2, blocking collectives, total_flow(): return lax.psum(local_sum, ('gx', 'gz')) / node_total  77.9 us
    ppermute x6, starting transfers between devices, extended(): lax.ppermute(lax.slice_in_dim(block, 0, width, axis=dim), axis, backward)  18.6 us
    unnamed x55, local copies, waits for them, and re-layouts  8.54 us
    ppermute x6, waiting for transfers between devices, extended(): lax.ppermute(lax.slice_in_dim(block, block.shape[dim] - width, None, axis...  7.44 us
    ppermute x6, waiting for transfers between devices, extended(): lax.ppermute(lax.slice_in_dim(block, 0, width, axis=dim), axis, backward)  6.59 us
    unnamed x78, other arithmetic  6.22 us
    concatenate x5, other arithmetic, extended(): block = jnp.concatenate([low, block, high], axis=dim)  3.06 us
  transfers between devices with their start and end apart: 12, of which 6 were waited for; matrix products, arithmetic and copies ran while one was open for 8% of the time, Pallas kernels for 0%

commit v1 on v0

--- a/solution.py
+++ b/solution.py
@@ -211,7 +211,7 @@
 
 
 def total_flow(local_sum, node_total):
-    return lax.psum(local_sum, ("gx", "gz")) / node_total
+    return lax.psum(lax.psum(local_sum, "gz"), "gx") / node_total
 
 
 def local(populations, solid, top_inflow):

time: 151 us -> 117 us (0.77)
  blocking collectives: 77.9 us -> 50 us
  starting transfers between devices: 20.7 us -> 17.8 us
  waiting for transfers between devices: 14 us -> 11.4 us
    psum x2 -> x4, blocking collectives: 77.9 us -> 50 us  [total_flow(): return lax.psum(lax.psum(local_sum, 'gz'), 'gx') / node_total]
    ppermute x6, starting transfers between devices: 18.6 us -> 14.2 us  [extended(): lax.ppermute(lax.slice_in_dim(block, 0, width, axis=dim), axis, backward)]
    ppermute x6, waiting for transfers between devices: 7.44 us -> 5.08 us  [extended(): lax.ppermute(lax.slice_in_dim(block, block.shape[dim] - width, None, axis...]
    ppermute x6, starting transfers between devices: 2.07 us -> 3.64 us  [extended(): lax.ppermute(lax.slice_in_dim(block, block.shape[dim] - width, None, axis...]
  transfers between devices with their start and end apart: 12 -> 12, of which waited for: 6 -> 7; matrix products, arithmetic and copies ran while one was open for 8% -> 10% of each run, Pallas kernels for 0% -> 0%
where the time goes in v1:
time: 117 us; the launch traced here: 116 us
  blocking collectives  50 us (43%)
  local copies, waits for them, and re-layouts  17.8 us (15%)
  starting transfers between devices  17.8 us (15%)
  other arithmetic  14.9 us (13%)
  waiting for transfers between devices  11.4 us (10%)
  matrix products  2.11 us (2%)
  between operations  2.08 us (2%)
    psum x4, blocking collectives, total_flow(): return lax.psum(lax.psum(local_sum, 'gz'), 'gx') / node_total  50 us
    ppermute x6, starting transfers between devices, extended(): lax.ppermute(lax.slice_in_dim(block, 0, width, axis=dim), axis, backward)  14.2 us
    unnamed x55, local copies, waits for them, and re-layouts  8.54 us
    ppermute x6, waiting for transfers between devices, extended(): lax.ppermute(lax.slice_in_dim(block, 0, width, axis=dim), axis, backward)  6.28 us
    unnamed x78, other arithmetic  6.22 us
    ppermute x6, waiting for transfers between devices, extended(): lax.ppermute(lax.slice_in_dim(block, block.shape[dim] - width, None, axis...  5.08 us
    ppermute x6, starting transfers between devices, extended(): lax.ppermute(lax.slice_in_dim(block, block.shape[dim] - width, None, axis...  3.64 us
    concatenate x5, other arithmetic, extended(): block = jnp.concatenate([low, block, high], axis=dim)  3.03 us
  transfers between devices with their start and end apart: 12, of which 7 were waited for; matrix products, arithmetic and copies ran while one was open for 10% of the time, Pallas kernels for 0%

profile of v1, /device:TPU:0, one launch (start us, length us, event | category | flops | bytes accessed | tf_op | source)
XLA Modules:
  0.0 116.1 jit_solution(10198862536636841309)
XLA Ops:
  1.0 4.5 %collective-permute-start.2 = (s32[8,8,1]{2,1,0:T(8,128)S(1)}, s32[8,8,1]{2,1,0:T(8,128)S(1)}, u32[]{:S(2)}, u32[]{:S(2)}) collective-permute-start(s32[8,8,1]{2,1,0:T(8,128)S(1)} %get-tuple-element.284), channel_id=1, source_target_pairs={{4,0},{8,4},{12,8},{16,12},{20,16},{24,20},{28,24},{0,28},{5,1},{9... | collective-permute-start | bytes 776 | tf_op jit(solution)/shard_map/ppermute | solution.py:49
  5.5 1.5 %fusion.243 = (f32[]{:T(128)}, f32[1,8,8,128]{3,2,1,0:T(8,128)S(1)}) fusion(s32[8,8,128]{2,1,0:T(8,128)S(1)} %copy-done.1, f32[19,8,8,128]{3,2,1,0:T(8,128)} %param.25), kind=kLoop, calls=%fused_computation.503 | loop fusion | flops 106495 | bytes 393220 | tf_op jit(solution)/shard_map/reduce_sum | solution.py:230
  7.0 10.5 %psum.28 = f32[]{:T(128)} all-reduce(f32[]{:T(128)} %get-tuple-element.179), channel_id=1, replica_groups=mesh['gx'=8,'gz'=4] {'gz'}, use_global_device_ids=true, to_apply=%region_2.0 | all-reduce | flops 1 | bytes 8 | tf_op jit(solution)/shard_map/psum | solution.py:214
  17.6 1.1 reduce_sum.40
  18.7 15.7 %psum.29 = f32[]{:T(128)} all-reduce(f32[]{:T(128)} %psum.28), channel_id=1, replica_groups=mesh['gx'=8,'gz'=4] {'gx'}, use_global_device_ids=true, to_apply=%region_3.0 | all-reduce | flops 1 | bytes 8 | tf_op jit(solution)/shard_map/psum | solution.py:214
  36.6 1.1 fusion.2
  38.1 1.2 copy.80
  39.8 3.6 %collective-permute-start.3 = (f32[19,8,8,1]{0,2,3,1:T(8,128)S(1)}, f32[19,8,8,1]{0,2,3,1:T(8,128)S(1)}, u32[]{:S(2)}, u32[]{:S(2)}) collective-permute-start(f32[19,8,8,1]{0,2,3,1:T(8,128)S(1)} %copy.82), channel_id=1, source_target_pairs={{4,0},{8,4},{12,8},{16,12},{20,16},{24,20},{28,24},{0,28},{5,1},{9... | collective-permute-start | bytes 14600 | tf_op jit(solution)/shard_map/ppermute | solution.py:49
  44.1 1.5 %collective-permute-start.4 = (s32[8,1,130]{2,1,0:T(1,128)S(1)}, s32[8,1,130]{2,1,0:T(1,128)S(1)}, u32[]{:S(2)}, u32[]{:S(2)}) collective-permute-start(s32[8,1,130]{2,1,0:T(1,128)S(1)} %get-tuple-element.243), channel_id=1, source_target_pairs={{0,1},{1,2},{2,3},{3,0},{4,5},{5,6},{6,7},{7,4},{8,9},{9,10},{10,1... | collective-permute-start | bytes 12488 | tf_op jit(solution)/shard_map/ppermute | solution.py:46
  47.3 1.4 %collective-permute-done.4 = s32[8,1,130]{2,1,0:T(1,128)S(1)} collective-permute-done((s32[8,1,130]{2,1,0:T(1,128)S(1)}, s32[8,1,130]{2,1,0:T(1,128)S(1)}, u32[]{:S(2)}, u32[]{:S(2)}) %collective-permute-start.4) | collective-permute-done | bytes 4192 | tf_op jit(solution)/shard_map/ppermute | solution.py:46
  50.3 1.5 %copy.81 = f32[19,8,8,1]{3,2,1,0:T(8,128)S(1)} copy(f32[19,8,8,1]{0,2,3,1:T(8,128)} %collective-permute-done.1) | data formatting | bytes 9728 | tf_op jit(solution)/shard_map/ppermute | solution.py:46
  51.9 1.0 pad_maximum_fusion.3
  54.3 1.4 %collective-permute-start.5 = (f32[19,8,1,130]{3,2,1,0:T(1,128)S(1)}, f32[19,8,1,130]{3,2,1,0:T(1,128)S(1)}, u32[]{:S(2)}, u32[]{:S(2)}) collective-permute-start(f32[19,8,1,130]{3,2,1,0:T(1,128)S(1)} %get-tuple-element.198), channel_id=1, source_target_pairs={{0,1},{1,2},{2,3},{3,0},{4,5},{5,6},{6,7},{7,4},{8,9},{9,10},{10,1... | collective-permute-start | bytes 237128 | tf_op jit(solution)/shard_map/ppermute | solution.py:46
  56.3 2.6 %collective-permute-done.7 = f32[19,8,1,130]{3,2,1,0:T(1,128)S(1)} collective-permute-done((f32[19,8,1,130]{3,2,1,0:T(1,128)S(1)}, f32[19,8,1,130]{3,2,1,0:T(1,128)S(1)}, u32[]{:S(2)}, u32[]{:S(2)}) %collective-permute-start.7) | collective-permute-done | bytes 79072 | tf_op jit(solution)/shard_map/ppermute | solution.py:49
  58.9 1.7 %collective-permute-done.5 = f32[19,8,1,130]{3,2,1,0:T(1,128)S(1)} collective-permute-done((f32[19,8,1,130]{3,2,1,0:T(1,128)S(1)}, f32[19,8,1,130]{3,2,1,0:T(1,128)S(1)}, u32[]{:S(2)}, u32[]{:S(2)}) %collective-permute-start.5) | collective-permute-done | bytes 79072 | tf_op jit(solution)/shard_map/ppermute | solution.py:46
  68.1 9.6 %psum.30 = f32[]{:T(128)} all-reduce(f32[]{:T(128)} %get-tuple-element.131), channel_id=1, replica_groups=mesh['gx'=8,'gz'=4] {'gz'}, use_global_device_ids=true, to_apply=%region_6.7 | all-reduce | flops 1 | bytes 8 | tf_op jit(solution)/shard_map/psum | solution.py:214
  77.6 14.2 %psum.31 = f32[]{:T(128)} all-reduce(f32[]{:T(128)} %psum.30), channel_id=1, replica_groups=mesh['gx'=8,'gz'=4] {'gx'}, use_global_device_ids=true, to_apply=%region_7.8 | all-reduce | flops 1 | bytes 8 | tf_op jit(solution)/shard_map/psum | solution.py:214
  94.0 1.1 fusion
  96.7 3.5 %collective-permute-start.9 = (f32[19,8,8,1]{0,2,3,1:T(8,128)S(1)}, f32[19,8,8,1]{0,2,3,1:T(8,128)S(1)}, u32[]{:S(2)}, u32[]{:S(2)}) collective-permute-start(f32[19,8,8,1]{0,2,3,1:T(8,128)S(1)} %copy.90), channel_id=1, source_target_pairs={{4,0},{8,4},{12,8},{16,12},{20,16},{24,20},{28,24},{0,28},{5,1},{9... | collective-permute-start | bytes 14600 | tf_op jit(solution)/shard_map/ppermute | solution.py:49
  100.8 1.0 collective-permute-done.9
  103.4 1.0 pad_maximum_fusion
  104.4 1.4 %collective-permute-start.11 = (f32[19,8,1,130]{3,2,1,0:T(1,128)S(1)}, f32[19,8,1,130]{3,2,1,0:T(1,128)S(1)}, u32[]{:S(2)}, u32[]{:S(2)}) collective-permute-start(f32[19,8,1,130]{3,2,1,0:T(1,128)S(1)} %get-tuple-element.193), channel_id=1, source_target_pairs={{1,0},{2,1},{3,2},{0,3},{5,4},{6,5},{7,6},{4,7},{9,8},{10,9},{11,1... | collective-permute-start | bytes 237128 | tf_op jit(solution)/shard_map/ppermute | solution.py:49
  107.9 2.5 %collective-permute-done.11 = f32[19,8,1,130]{3,2,1,0:T(1,128)S(1)} collective-permute-done((f32[19,8,1,130]{3,2,1,0:T(1,128)S(1)}, f32[19,8,1,130]{3,2,1,0:T(1,128)S(1)}, u32[]{:S(2)}, u32[]{:S(2)}) %collective-permute-start.11) | collective-permute-done | bytes 79072 | tf_op jit(solution)/shard_map/ppermute | solution.py:49
  110.4 2.0 %collective-permute-done.10 = f32[19,8,1,130]{3,2,1,0:T(1,128)S(1)} collective-permute-done((f32[19,8,1,130]{3,2,1,0:T(1,128)S(1)}, f32[19,8,1,130]{3,2,1,0:T(1,128)S(1)}, u32[]{:S(2)}, u32[]{:S(2)}) %collective-permute-start.10) | collective-permute-done | bytes 79072 | tf_op jit(solution)/shard_map/ppermute | solution.py:46
  (180 shorter events, 27.4 us)
Async XLA Ops:
  0.0 5.5 %copy-start.1 = (s32[8,8,128]{2,1,0:T(8,128)S(1)}, s32[8,8,128]{2,1,0:T(8,128)}, u32[]{:S(2)}) copy-start(s32[8,8,128]{2,1,0:T(8,128)} %param.26) | copy-start | bytes 98308
  0.0 35.1 %copy-start = (f32[19,8,8,128]{3,2,1,0:T(8,128)S(1)}, f32[19,8,8,128]{3,2,1,0:T(8,128)}, u32[]{:S(2)}) copy-start(f32[19,8,8,128]{3,2,1,0:T(8,128)} %param.25) | copy-start | bytes 1867780
  1.0 42.5 %collective-permute-start.2 = (s32[8,8,1]{2,1,0:T(8,128)S(1)}, s32[8,8,1]{2,1,0:T(8,128)S(1)}, u32[]{:S(2)}, u32[]{:S(2)}) collective-permute-start(s32[8,8,1]{2,1,0:T(8,128)S(1)} %get-tuple-element.284), channel_id=1, source_target_pairs={{4,0},{8,4},{12,8},{16,12},{20,16},{24,20},{28,24},{0,28},{5,1},{9... | collective-permute-start | bytes 776 | tf_op jit(solution)/shard_map/ppermute | solution.py:49
  5.5 37.9 %collective-permute-start = (s32[8,8,1]{2,1,0:T(8,128)S(1)}, s32[8,8,1]{2,1,0:T(8,128)S(1)}, u32[]{:S(2)}, u32[]{:S(2)}) collective-permute-start(s32[8,8,1]{2,1,0:T(8,128)S(1)} %get-tuple-element.285), channel_id=1, source_target_pairs={{0,4},{4,8},{8,12},{12,16},{16,20},{20,24},{24,28},{28,0},{1,5},{5... | collective-permute-start | bytes 776 | tf_op jit(solution)/shard_map/ppermute | solution.py:46
  39.3 11.0 %collective-permute-start.1 = (f32[19,8,8,1]{0,2,3,1:T(8,128)}, f32[19,8,8,1]{0,2,3,1:T(8,128)}, u32[]{:S(2)}, u32[]{:S(2)}) collective-permute-start(f32[19,8,8,1]{0,2,3,1:T(8,128)} %copy.80), channel_id=1, source_target_pairs={{0,4},{4,8},{8,12},{12,16},{16,20},{20,24},{24,28},{28,0},{1,5},{5... | collective-permute-start | bytes 14600 | tf_op jit(solution)/shard_map/ppermute | solution.py:46
  39.8 9.7 %collective-permute-start.3 = (f32[19,8,8,1]{0,2,3,1:T(8,128)S(1)}, f32[19,8,8,1]{0,2,3,1:T(8,128)S(1)}, u32[]{:S(2)}, u32[]{:S(2)}) collective-permute-start(f32[19,8,8,1]{0,2,3,1:T(8,128)S(1)} %copy.82), channel_id=1, source_target_pairs={{4,0},{8,4},{12,8},{16,12},{20,16},{24,20},{28,24},{0,28},{5,1},{9... | collective-permute-start | bytes 14600 | tf_op jit(solution)/shard_map/ppermute | solution.py:49
  43.6 3.7 %collective-permute-start.6 = (s32[8,1,130]{2,1,0:T(1,128)S(1)}, s32[8,1,130]{2,1,0:T(1,128)S(1)}, u32[]{:S(2)}, u32[]{:S(2)}) collective-permute-start(s32[8,1,130]{2,1,0:T(1,128)S(1)} %get-tuple-element.242), channel_id=1, source_target_pairs={{1,0},{2,1},{3,2},{0,3},{5,4},{6,5},{7,6},{4,7},{9,8},{10,9},{11,1... | collective-permute-start | bytes 12488 | tf_op jit(solution)/shard_map/ppermute | solution.py:49
  44.1 4.5 %collective-permute-start.4 = (s32[8,1,130]{2,1,0:T(1,128)S(1)}, s32[8,1,130]{2,1,0:T(1,128)S(1)}, u32[]{:S(2)}, u32[]{:S(2)}) collective-permute-start(s32[8,1,130]{2,1,0:T(1,128)S(1)} %get-tuple-element.243), channel_id=1, source_target_pairs={{0,1},{1,2},{2,3},{3,0},{4,5},{5,6},{6,7},{7,4},{8,9},{9,10},{10,1... | collective-permute-start | bytes 12488 | tf_op jit(solution)/shard_map/ppermute | solution.py:46
  53.0 2.7 %copy-start.12 = (s32[7,8,128]{2,1,0:T(8,128)S(1)}, s32[7,8,128]{2,1,0:T(8,128)}, u32[]{:S(2)}) copy-start(s32[7,8,128]{2,1,0:T(8,128)} %get-tuple-element.282) | copy-start | bytes 86020
  53.7 5.2 %collective-permute-start.7 = (f32[19,8,1,130]{3,2,1,0:T(1,128)S(1)}, f32[19,8,1,130]{3,2,1,0:T(1,128)S(1)}, u32[]{:S(2)}, u32[]{:S(2)}) collective-permute-start(f32[19,8,1,130]{3,2,1,0:T(1,128)S(1)} %get-tuple-element.197), channel_id=1, source_target_pairs={{1,0},{2,1},{3,2},{0,3},{5,4},{6,5},{7,6},{4,7},{9,8},{10,9},{11,1... | collective-permute-start | bytes 237128 | tf_op jit(solution)/shard_map/ppermute | solution.py:49
  54.3 6.3 %collective-permute-start.5 = (f32[19,8,1,130]{3,2,1,0:T(1,128)S(1)}, f32[19,8,1,130]{3,2,1,0:T(1,128)S(1)}, u32[]{:S(2)}, u32[]{:S(2)}) collective-permute-start(f32[19,8,1,130]{3,2,1,0:T(1,128)S(1)} %get-tuple-element.198), channel_id=1, source_target_pairs={{0,1},{1,2},{2,3},{3,0},{4,5},{5,6},{6,7},{7,4},{8,9},{9,10},{10,1... | collective-permute-start | bytes 237128 | tf_op jit(solution)/shard_map/ppermute | solution.py:46
  60.6 0.7 copy-start.6
  60.6 0.8 copy-start.7
  60.6 0.8 copy-start.8
  60.6 0.8 copy-start.10
  60.6 0.8 copy-start.11
  62.9 0.7 copy-start.9
  65.8 0.7 copy-start.4
  66.6 0.7 copy-start.3
  96.6 5.9 %collective-permute-start.8 = (f32[19,8,8,1]{0,2,3,1:T(8,128)S(1)}, f32[19,8,8,1]{0,2,3,1:T(8,128)S(1)}, u32[]{:S(2)}, u32[]{:S(2)}) collective-permute-start(f32[19,8,8,1]{0,2,3,1:T(8,128)S(1)} %copy.88), channel_id=1, source_target_pairs={{0,4},{4,8},{8,12},{12,16},{16,20},{20,24},{24,28},{28,0},{1,5},{5... | collective-permute-start | bytes 14600 | tf_op jit(solution)/shard_map/ppermute | solution.py:46
  96.7 5.1 %collective-permute-start.9 = (f32[19,8,8,1]{0,2,3,1:T(8,128)S(1)}, f32[19,8,8,1]{0,2,3,1:T(8,128)S(1)}, u32[]{:S(2)}, u32[]{:S(2)}) collective-permute-start(f32[19,8,8,1]{0,2,3,1:T(8,128)S(1)} %copy.90), channel_id=1, source_target_pairs={{4,0},{8,4},{12,8},{16,12},{20,16},{24,20},{28,24},{0,28},{5,1},{9... | collective-permute-start | bytes 14600 | tf_op jit(solution)/shard_map/ppermute | solution.py:49
  103.4 3.1 %copy-start.2 = (f32[19,8,8,128]{3,2,1,0:T(8,128)S(1)}, f32[19,8,8,128]{3,2,1,0:T(8,128)}, u32[]{:S(2)}) copy-start(f32[19,8,8,128]{3,2,1,0:T(8,128)} %constant_dynamic-update-slice_fusion.115) | copy-start | bytes 1867780
  104.4 6.0 %collective-permute-start.11 = (f32[19,8,1,130]{3,2,1,0:T(1,128)S(1)}, f32[19,8,1,130]{3,2,1,0:T(1,128)S(1)}, u32[]{:S(2)}, u32[]{:S(2)}) collective-permute-start(f32[19,8,1,130]{3,2,1,0:T(1,128)S(1)} %get-tuple-element.193), channel_id=1, source_target_pairs={{1,0},{2,1},{3,2},{0,3},{5,4},{6,5},{7,6},{4,7},{9,8},{10,9},{11,1... | collective-permute-start | bytes 237128 | tf_op jit(solution)/shard_map/ppermute | solution.py:49
  105.8 6.6 %collective-permute-start.10 = (f32[19,8,1,130]{3,2,1,0:T(1,128)S(1)}, f32[19,8,1,130]{3,2,1,0:T(1,128)S(1)}, u32[]{:S(2)}, u32[]{:S(2)}) collective-permute-start(f32[19,8,1,130]{3,2,1,0:T(1,128)S(1)} %get-tuple-element.194), channel_id=1, source_target_pairs={{0,1},{1,2},{2,3},{3,0},{4,5},{5,6},{6,7},{7,4},{8,9},{9,10},{10,1... | collective-permute-start | bytes 237128 | tf_op jit(solution)/shard_map/ppermute | solution.py:46
  (10 other events, 7.1 us)
